TPU v7x, 32 devices: a whole 2x2x4 slice. The times are simulated.
32 devices in a mesh: seq: 8 (over z, y), head: 4 (over x, core).
Axes of the slice: x: 2, y: 2, z: 4, core: 2. Of those that a mesh axis runs over, the one named last changes fastest.
Arguments:
- tokens: bfloat16 [6144, 2560], P(('seq', 'head')), may hold values from -12 to 12
- pre_gain: float32 [2560], replicated, may hold values from 0.25 to 1.75
- inner_proj: bfloat16 [2560, 2, 5120], P(None, None, 'head'), may hold values from -0.125 to 0.125
- outer_proj: bfloat16 [2560, 336], replicated, may hold values from -0.125 to 0.125
- kernel_x: float32 [4, 5120], P(None, 'head'), may hold values from -3 to 3
- kernel_bc: float32 [4, 256], replicated, may hold values from -3 to 3
- offset_x: float32 [5120], P('head'), may hold values from -3 to 3
- offset_bc: float32 [256], replicated, may hold values from -3 to 3
- dt_bias: float32 [80], P('head'), may hold values from -7 to -5
- a_log: float32 [80], P('head'), may hold values from -12 to 4
- skip_gain: float32 [80], P('head'), may hold values from 0.5 to 1.5
- norm_gain: float32 [5120], P('head'), may hold values from 0.25 to 1.75
- out_proj: bfloat16 [5120, 2560], P('head'), may hold values from -0.078125 to 0.078125
Outputs:
- mixed: bfloat16 [6144, 2560], P(('seq', 'head'))
All inputs are finite; a program needn't handle non-finite values.
Results may differ from a plain program's by a relative error of at most 0.014.
Values may be sent and summed in bfloat16 or wider, within the bound.
A program may use at most 128 MiB of HBM per device.

v0:
```python
import jax
import jax.numpy as jnp
from jax import lax
from jax.sharding import PartitionSpec as P

SPAN = 256


norm_floor = 0.1


def passed_along(block, axis, distance):
    devices = range(lax.axis_size(axis))
    route = [(i - distance, i) for i in devices if i - distance in devices]
    return lax.ppermute(block, axis, route)


def entering(array, axis, combine, identity):
    length, position = (lax.axis_size(axis), lax.axis_index(axis))
    everything = jax.tree.map(lambda part: lax.all_gather(part, axis), array)
    start = jax.tree.map(
        lambda part, zero: jnp.broadcast_to(jnp.asarray(zero, part.dtype), part.shape),
        array,
        identity,
    )

    def lap(k, before):
        reached = k < position
        new = combine(before, jax.tree.map(lambda part: part[k], everything))
        return jax.tree.map(lambda a, b: jnp.where(reached, a, b), new, before)

    return lax.fori_loop(0, length, lap, start)


def row_norm(row_block, gain_vector):
    widened = row_block.astype(jnp.float32)
    inverse_rms = lax.rsqrt(jnp.mean(widened * widened, axis=-1, keepdims=True) + norm_floor)
    return widened * inverse_rms * gain_vector


def masked_exp(log_gap, causal):
    return jnp.where(causal, jnp.exp(jnp.where(causal, log_gap, 0.0)), 0.0)


def on_device(
    tokens,
    pre_gain,
    inner_proj,
    outer_proj,
    kernel_x,
    kernel_bc,
    offset_x,
    offset_bc,
    dt_bias,
    a_log,
    skip_gain,
    norm_gain,
    out_proj,
):
    model_width = inner_proj.shape[0]
    local_width = inner_proj.shape[2]
    head_count = dt_bias.shape[0]
    head_size = local_width // head_count
    state_size = kernel_bc.shape[1] // 2
    kernel_size = kernel_x.shape[0]
    joined_proj = inner_proj.reshape(model_width, 2 * local_width)
    normed = row_norm(lax.all_gather(tokens, "head", axis=0, tiled=True), pre_gain).astype(
        jnp.bfloat16
    )
    inner_part = jnp.dot(normed, joined_proj, preferred_element_type=jnp.float32)
    outer_part = jnp.dot(normed, outer_proj, preferred_element_type=jnp.float32)
    projected = jnp.concatenate([inner_part, outer_part], axis=1)
    seq_rows = projected.shape[0]
    gate_in = projected[:, :local_width].astype(jnp.bfloat16)
    conv_input = projected[:, local_width : 2 * local_width + 2 * state_size].astype(jnp.bfloat16)
    head_index = lax.axis_index("head")
    dt_raw = lax.dynamic_slice_in_dim(
        projected[:, 2 * local_width + 2 * state_size :], head_index * head_count, head_count, 1
    )
    conv_tail = passed_along(conv_input[seq_rows - kernel_size + 1 :], "seq", 1)
    extended = jnp.concatenate([conv_tail, conv_input], axis=0)
    conv_weight = jnp.concatenate([kernel_x, kernel_bc], axis=1)
    conv_bias = jnp.concatenate([offset_x, offset_bc])
    summed = jnp.broadcast_to(conv_bias, conv_input.shape)
    for offset in range(kernel_size):
        summed = summed + conv_weight[offset] * extended[offset : offset + seq_rows].astype(
            jnp.float32
        )
    conv_out = jax.nn.silu(summed).astype(jnp.bfloat16)
    blocks = seq_rows // SPAN
    values_x = conv_out[:, :local_width].reshape(blocks, SPAN, head_count, head_size)
    values_b = conv_out[:, local_width : local_width + state_size].reshape(blocks, SPAN, state_size)
    values_c = conv_out[:, local_width + state_size :].reshape(blocks, SPAN, state_size)
    step_flat = jax.nn.softplus(dt_raw + dt_bias)
    log_rates = (step_flat * -jnp.exp(a_log)).reshape(blocks, SPAN, head_count)
    step_sizes = step_flat.reshape(blocks, SPAN, head_count)
    running = jnp.cumsum(log_rates, axis=1)
    score_rows = jnp.einsum("ctn,csn->cts", values_c, values_b, preferred_element_type=jnp.float32)
    running_heads = jnp.transpose(running, (0, 2, 1))
    steps_heads = jnp.transpose(step_sizes, (0, 2, 1))
    row_index = lax.broadcasted_iota(jnp.int32, (SPAN, SPAN), 0)
    col_index = lax.broadcasted_iota(jnp.int32, (SPAN, SPAN), 1)
    decay_factor = masked_exp(
        running_heads[:, :, :, None] - running_heads[:, :, None, :], row_index >= col_index
    )
    mix_weights = (score_rows[:, None] * decay_factor * steps_heads[:, :, None, :]).astype(
        jnp.bfloat16
    )
    intra_out = jnp.einsum(
        "chts,cshp->cthp", mix_weights, values_x, preferred_element_type=jnp.float32
    )
    end_weight = jnp.exp(running[:, -1:, :] - running) * step_sizes
    scaled_x = (values_x.astype(jnp.float32) * end_weight[..., None]).astype(jnp.bfloat16)
    block_states = jnp.einsum(
        "cshp,csn->chpn", scaled_x, values_b, preferred_element_type=jnp.float32
    )
    block_total = running[:, -1, :]
    prefix_rate = jnp.concatenate(
        [jnp.zeros((1, head_count), jnp.float32), jnp.cumsum(block_total, axis=0)], axis=0
    )
    prefix_heads = prefix_rate.T
    later_index = lax.broadcasted_iota(jnp.int32, (blocks + 1, blocks), 0)
    source_index = lax.broadcasted_iota(jnp.int32, (blocks + 1, blocks), 1)
    link_weight = masked_exp(
        prefix_heads[:, :, None] - prefix_heads[:, None, 1:], source_index < later_index
    )
    local_states = jnp.einsum(
        "hce,ehpn->chpn", link_weight, block_states, precision=lax.Precision.HIGHEST
    )
    summary = local_states[blocks]
    device_rate = prefix_rate[blocks]

    def combine(earlier_part, later_part):
        return (
            earlier_part[0] + later_part[0],
            jnp.exp(later_part[0])[:, None, None] * earlier_part[1] + later_part[1],
        )

    identity = (
        jnp.zeros((head_count,), jnp.float32),
        jnp.zeros((head_count, head_size, state_size), jnp.float32),
    )
    carried = entering((device_rate, summary), "seq", combine, identity)[1]
    block_inputs = (
        local_states[:blocks] + jnp.exp(prefix_rate[:blocks])[:, :, None, None] * carried[None]
    )
    cross_out = jnp.exp(running)[..., None] * jnp.einsum(
        "ctn,chpn->cthp",
        values_c.astype(jnp.float32),
        block_inputs,
        precision=lax.Precision.HIGHEST,
    )
    mixer_out = (intra_out + cross_out + skip_gain[:, None] * values_x.astype(jnp.float32)).reshape(
        seq_rows, local_width
    )
    gated = mixer_out * jax.nn.silu(gate_in.astype(jnp.float32))
    squares = lax.psum(jnp.sum(gated * gated, axis=1), "head")
    inverse_rms = lax.rsqrt(squares / (local_width * lax.axis_size("head")) + norm_floor)
    normed_out = (gated * inverse_rms[:, None] * norm_gain).astype(jnp.bfloat16)
    return lax.psum_scatter(
        jnp.dot(normed_out, out_proj, preferred_element_type=jnp.float32).astype(jnp.bfloat16),
        "head",
        scatter_dimension=0,
        tiled=True,
    )


def solution(mesh):
    return jax.shard_map(
        on_device,
        mesh=mesh,
        in_specs=(
            P(("seq", "head"), None),
            P(),
            P(None, None, "head"),
            P(),
            P(None, "head"),
            P(),
            P("head"),
            P(),
            P("head"),
            P("head"),
            P("head"),
            P("head"),
            P("head", None),
        ),
        out_specs=P(("seq", "head"), None),
        check_vma=False,
    )
```

profile of v0, /device:TPU:0, one launch (start us, length us, event | category | flops | bytes accessed | tf_op | source)
XLA Modules:
  0.0 299.9 jit_solution(3712569174115539609)
XLA Ops:
  7.4 12.5 %copy.105 = bf16[320,8,2,1280]{3,1,2,0:T(8,128)(2,1)} copy(bf16[320,8,2,1280]{3,2,1,0:T(2,128)(2,1)} %bitcast.58) | data formatting | bytes 26214400
  20.0 24.6 %all-gather.4.cloned.1.call-done = bf16[768,2560]{1,0:T(8,128)(2,1)} async-done(((bf16[192,2560]{1,0:T(8,128)(2,1)}), bf16[768,2560]{1,0:T(8,128)(2,1)}) %all-gather.4.cloned.1.call-update) | async-done | bytes 3932176 | tf_op jit(solution)/shard_map/all_gather | solution.py:67
  44.6 3.1 %fusion.2 = f32[768]{0:T(1024)S(1)} fusion(bf16[768,2560]{1,0:T(8,128)(2,1)} %all-gather.4.cloned.1.call-done), kind=kLoop, calls=%fused_computation.7 | loop fusion | flops 5897472 | bytes 3935232 | tf_op jit(solution)/shard_map/reduce_sum | solution.py:37
  47.9 1.6 fusion.47
  49.8 14.7 %convolution_convert_fusion.1 = bf16[768,2560]{1,0:T(8,128)(2,1)S(1)} fusion(bf16[2560,2560]{1,0:T(8,128)(2,1)} %bitcast.59, bf16[768,2560]{1,0:T(8,128)(2,1)} %all-gather.4.cloned.1.call-done, f32[2560]{0:T(1024)S(1)} %copy-done.11, f32[768]{0:T(1024)S(1)} %add_rsqrt_fusion.1), kind=kOutput, calls=%fused_computation.17 | convolution fusion | flops 10076160000 | bytes 20984832 | tf_op jit(solution)/shard_map/dot_general | solution.py:70
  64.5 1.7 pad_maximum_fusion.1
  67.5 1.7 reduce-window.6
  70.0 3.6 %collective-permute-start = (bf16[3,1536]{1,0:T(4,128)(2,1)S(1)}, bf16[3,1536]{1,0:T(4,128)(2,1)S(1)}, u32[]{:S(2)}, u32[]{:S(2)}) collective-permute-start(bf16[3,1536]{1,0:T(4,128)(2,1)S(1)} %pad_maximum_fusion.2), channel_id=1, source_target_pairs={{0,4},{4,8},{8,12},{12,16},{16,20},{20,24},{24,28},{1,5},{5,9},{9,... | collective-permute-start | bytes 27656 | tf_op jit(solution)/shard_map/ppermute | solution.py:15
  74.8 7.0 %multiply_convert_fusion.2 = bf16[768,1536]{1,0:T(8,128)(2,1)S(1)} fusion(bf16[768,1536]{1,0:T(8,128)(2,1)} %pad_maximum_fusion.1, bf16[3,1536]{1,0:T(4,128)(2,1)S(1)} %collective-permute-done, f32[1536]{0:T(1024)S(1)} %get-tuple-element.134, f32[1536]{0:T(1024)S(1)} %get-tuple-element.135, f32[1536]{0:T(1024)S(1)} %get-tuple-element.136, ...), kind=kLoop, calls=%fused_computation.22 | loop fusion | flops 30670848 | bytes 4758528 | tf_op jit(solution)/shard_map/convert_element_type | solution.py:89
  81.9 1.4 slice.100
  83.3 6.6 %reshape.98 = bf16[3,256,20,64]{3,2,1,0:T(8,128)(2,1)} reshape(bf16[768,1280]{1,0:T(8,128)(2,1)} %slice.100) | data formatting | bytes 3932160 | tf_op jit(solution)/shard_map/reshape | solution.py:91
  89.9 6.2 %copy.85 = bf16[3,256,20,64]{1,3,2,0:T(8,128)(2,1)} copy(bf16[3,256,20,64]{3,2,1,0:T(8,128)(2,1)} %reshape.98) | data formatting | bytes 3932160 | tf_op jit(solution)/shard_map/reshape | solution.py:91
  96.1 2.2 fusion.21
  98.3 5.6 %fusion.28 = f32[4,20,64,128]{3,0,2,1:T(4,128)S(1)} fusion(f32[3,20,64,128]{3,2,1,0:T(8,128)S(1)} %fusion.21, f32[20,3]{1,0:T(8,128)S(1)} %copy.89, f32[20,4]{1,0:T(8,128)S(1)} %copy.88, pred[4,3]{1,0:T(4,128)(4,1)S(1)} %iota_compare_fusion.1), kind=kOutput, calls=%fused_computation.47 | convolution fusion | flops 23593680 | bytes 4588092 | tf_op jit(solution)/shard_map/hce,ehpn->chpn/dot_general | solution.py:127
  104.0 1.5 copy-done.3
  105.5 1.5 slice.108
  107.3 21.9 %all-gather = f32[8,1,20]{2,1,0:T(1,128)S(1)} all-gather(f32[1,1,20]{2,1,0:T(1,128)S(1)} %slice_bitcast_fusion), channel_id=1, replica_groups=mesh['seq'=8,'head'=4] {'seq'}, dimensions={0}, use_global_device_ids=true | all-gather | bytes 720 | tf_op jit(solution)/shard_map/all_gather | solution.py:20
  129.4 64.5 %all-gather.6.cloned.1.call-done = f32[8,20,64,128]{3,2,1,0:T(8,128)} async-done(((f32[1,20,64,128]{3,2,1,0:T(8,128)}), f32[8,20,64,128]{3,2,1,0:T(8,128)}) %all-gather.6.cloned.1.call-update) | async-done | bytes 5242896 | tf_op jit(solution)/shard_map/all_gather | solution.py:20
  193.9 10.2 %while.14 = (s32[]{:T(128)}, f32[20,64,128]{2,1,0:T(8,128)S(1)}, s32[]{:T(128)}, f32[8,20]{1,0:T(8,128)S(1)}, f32[8,20,64,128]{3,2,1,0:T(8,128)}, /*index=5*/s32[]{:T(128)}, s32[]{:T(128)}) while((s32[]{:T(128)}, f32[20,64,128]{2,1,0:T(8,128)S(1)}, s32[]{:T(128)}, f32[8,20]{1,0:T(8,128)S(1)}, f32[8,20,64,128]{3,2,1,0:T(8,128)}, ...), condition=%wide.region_5.6_spmd.clone, body=%wide.region_4.5_spmd.clone.sunk | while | flops 655364 | bytes 1966425 | solution.py:32
  193.9 1.2 fusion.58
  200.3 1.2 fusion.58
  201.6 1.2 fusion.58
  202.9 1.2 fusion.58
  204.1 2.6 slice_add_fusion
  206.7 1.8 fusion.23
  208.5 6.6 %fusion.12 = f32[3,256,20,64]{1,3,2,0:T(8,128)} fusion(bf16[3,256,20,64]{1,3,2,0:T(8,128)(2,1)S(1)} %copy-done.4, f32[3,256,20,64]{1,3,2,0:T(8,128)S(1)} %fusion.23, f32[3,20,256]{2,1,0:T(8,128)S(1)} %copy.84, f32[3,20,256]{2,1,0:T(8,128)S(1)} %reduce_window_sum.35, f32[3,256,256]{2,1,0:T(8,128)S(1)} %fusion.48, pred[256,256]{1,0:T(8,128)(4,1)S(1)} %iota_compare_fusion, ...), kind=kOutput, calls=%fused_computation.24 | convolution fusion | flops 531824640 | bytes 10866768 | tf_op jit(solution)/shard_map/chts,cshp->cthp/dot_general | solution.py:109
  215.1 7.9 %copy.101 = f32[3,256,20,64]{3,2,1,0:T(8,128)} copy(f32[3,256,20,64]{1,3,2,0:T(8,128)} %fusion.12) | data formatting | bytes 7864320 | tf_op jit(solution)/shard_map/reshape | solution.py:153
  223.0 7.6 %reshape.97 = f32[768,1280]{1,0:T(8,128)} reshape(f32[3,256,20,64]{3,2,1,0:T(8,128)} %copy.101) | data formatting | bytes 7864320 | tf_op jit(solution)/shard_map/reshape | solution.py:153
  230.6 4.0 %multiply_reduce_fusion = f32[768]{0:T(1024)S(1)} fusion(f32[768,1280]{1,0:T(8,128)} %reshape.97, bf16[768,2560]{1,0:T(8,128)(2,1)} %copy-done.2), kind=kLoop, calls=%fused_computation.31 | loop fusion | flops 7863552 | bytes 5901312 | tf_op jit(solution)/shard_map/reduce_sum | solution.py:157
  234.6 5.7 %psum.7 = f32[768]{0:T(1024)S(1)} all-reduce(f32[768]{0:T(1024)S(1)} %multiply_reduce_fusion), channel_id=1, replica_groups=mesh['seq'=8,'head'=4] {'head'}, use_global_device_ids=true, to_apply=%region_7.8 | all-reduce | flops 768 | bytes 6144 | tf_op jit(solution)/shard_map/psum | solution.py:157
  240.3 11.5 %convolution_convert_fusion = bf16[768,2560]{1,0:T(8,128)(2,1)} fusion(bf16[1280,2560]{1,0:T(8,128)(2,1)} %param.27, f32[1280]{0:T(1024)S(1)} %copy-done.12, f32[768]{0:T(1024)S(1)} %add_rsqrt_fusion, f32[768,1280]{1,0:T(8,128)} %reshape.97, bf16[768,2560]{1,0:T(8,128)(2,1)} %copy-done.2), kind=kOutput, calls=%fused_computation.16 | convolution fusion | flops 5043978240 | bytes 16392192 | tf_op jit(solution)/shard_map/dot_general | solution.py:161
  251.8 41.5 %reduce-scatter.2.cloned.1.call-done = bf16[192,2560]{1,0:T(8,128)(2,1)} async-done(((bf16[768,2560]{1,0:T(8,128)(2,1)}), bf16[192,2560]{1,0:T(8,128)(2,1)}) %reduce-scatter.2.cloned.1.call-update) | async-done | bytes 983056 | tf_op jit(solution)/shard_map/reduce_scatter | solution.py:160
  (85 shorter events, 10.1 us)
Async XLA Ops:
  6.5 41.2 %copy-start = (bf16[2560,336]{0,1:T(8,128)(2,1)S(1)}, bf16[2560,336]{0,1:T(8,128)(2,1)}, u32[]{:S(2)}) copy-start(bf16[2560,336]{0,1:T(8,128)(2,1)} %param.18) | copy-start | bytes 5160964
  6.5 38.1 %all-gather.4.cloned.1.call-start = ((), (), s32[]{:S(2)}) async-start(), calls=%async_computation.1 | async-start | bytes 4915200 | tf_op jit(solution)/shard_map/all_gather | solution.py:67
  7.3 186.7 %all-gather.6.cloned.1.call-start = ((), (), s32[]{:S(2)}) async-start(), calls=%async_computation.2 | async-start | bytes 5898240 | tf_op jit(solution)/shard_map/all_gather | solution.py:20
  7.3 12.5 %copy-start.6 = (f32[4,1280]{1,0:T(4,128)S(1)}, f32[4,1280]{1,0:T(4,128)}, u32[]{:S(2)}) copy-start(f32[4,1280]{1,0:T(4,128)} %param.19) | copy-start | bytes 61444
  7.3 12.5 %copy-start.8 = (f32[4,256]{1,0:T(4,128)S(1)}, f32[4,256]{1,0:T(4,128)}, u32[]{:S(2)}) copy-start(f32[4,256]{1,0:T(4,128)} %param.20) | copy-start | bytes 12292
  7.3 12.6 %copy-start.7 = (f32[1280]{0:T(1024)S(1)}, f32[1280]{0:T(1024)}, u32[]{:S(2)}) copy-start(f32[1280]{0:T(1024)} %param.21) | copy-start | bytes 15364
  7.3 12.6 %copy-start.9 = (f32[256]{0:T(256)S(1)}, f32[256]{0:T(256)}, u32[]{:S(2)}) copy-start(f32[256]{0:T(256)} %param.22) | copy-start | bytes 3076
  7.4 12.6 %copy-start.13 = (f32[20]{0:T(128)S(1)}, f32[20]{0:T(128)}, u32[]{:S(2)}) copy-start(f32[20]{0:T(128)} %param.24) | copy-start | bytes 244
  19.8 27.9 %copy-start.11 = (f32[2560]{0:T(1024)S(1)}, f32[2560]{0:T(1024)}, u32[]{:S(2)}) copy-start(f32[2560]{0:T(1024)} %param.16) | copy-start | bytes 30724
  44.6 3.3 %copy-start.5 = (bf16[768,2560]{1,0:T(8,128)(2,1)S(1)}, bf16[768,2560]{1,0:T(8,128)(2,1)}, u32[]{:S(2)}) copy-start(bf16[768,2560]{1,0:T(8,128)(2,1)} %all-gather.4.cloned.1.call-done) | copy-start | bytes 11796484
  64.5 2.7 copy-start.2
  66.2 1.1 copy-start.10
  70.0 4.8 %collective-permute-start = (bf16[3,1536]{1,0:T(4,128)(2,1)S(1)}, bf16[3,1536]{1,0:T(4,128)(2,1)S(1)}, u32[]{:S(2)}, u32[]{:S(2)}) collective-permute-start(bf16[3,1536]{1,0:T(4,128)(2,1)S(1)} %pad_maximum_fusion.2), channel_id=1, source_target_pairs={{0,4},{4,8},{8,12},{12,16},{16,20},{20,24},{24,28},{1,5},{5,9},{9,... | collective-permute-start | bytes 27656 | tf_op jit(solution)/shard_map/ppermute | solution.py:15
  104.0 1.5 copy-start.3
  107.1 186.3 %reduce-scatter.2.cloned.1.call-start = ((), (), s32[]{:S(2)}) async-start(), calls=%async_computation.3 | async-start | bytes 4915200 | tf_op jit(solution)/shard_map/reduce_scatter | solution.py:160
  206.7 1.8 copy-start.4
  206.7 1.8 copy-start.14
  230.6 9.7 %copy-start.12 = (f32[1280]{0:T(1024)S(1)}, f32[1280]{0:T(1024)}, u32[]{:S(2)}) copy-start(f32[1280]{0:T(1024)} %param.26) | copy-start | bytes 15364
  240.3 53.0 %copy-start.1 = (bf16[2560,336]{0,1:T(8,128)(2,1)S(1)}, bf16[2560,336]{0,1:T(8,128)(2,1)}, u32[]{:S(2)}) copy-start(bf16[2560,336]{0,1:T(8,128)(2,1)} %param.18) | copy-start | bytes 5160964
Sparse Core Ops, SparseCore 0:
  8.9 35.6 all-gather.3
  107.2 86.7 all-gather.5
  251.9 41.3 reduce-scatter.1
where the time goes:
time: 301 us; the launch traced here: 300 us
  waiting for transfers between devices  132 us (44%)
  local copies, waits for them, and re-layouts  47.9 us (16%)
  matrix products  44.2 us (15%)
  other arithmetic  30.4 us (10%)
  blocking collectives  27.6 us (9%)
  between operations  13.5 us (4%)
  starting transfers between devices  3.65 us (1%)
    all_gather x1, waiting for transfers between devices, entering(): everything = jax.tree.map(lambda part: lax.all_gather(part, axis), array)  64.5 us
    reduce_scatter x1, waiting for transfers between devices, on_device(): lax.psum_scatter(jnp.dot(normed_out, out_proj, preferred_element_type=jnp...  41.5 us
    all_gather x1, waiting for transfers between devices, on_device(): lax.all_gather(tokens, 'head', axis=0, tiled=True)  24.6 us
    all_gather x1, blocking collectives, entering(): everything = jax.tree.map(lambda part: lax.all_gather(part, axis), array)  21.9 us
    reshape x2, local copies, waits for them, and re-layouts, on_device(): (intra_out + cross_out + skip_gain[:, None] * values_x.astype(jnp.float32...  15.5 us
    unnamed x33, local copies, waits for them, and re-layouts  15.2 us
    dot_general x1, matrix products, on_device(): jnp.dot(normed, joined_proj, preferred_element_type=jnp.float32)  14.7 us
    reshape x2, local copies, waits for them, and re-layouts, on_device(): conv_out[:, :local_width].reshape(blocks, SPAN, head_count, head_size)  12.8 us
  transfers between devices with their start and end apart: 4, of which 4 were waited for; matrix products, arithmetic and copies ran while one was open for 4% of the time, Pallas kernels for 0%

commit v1 on v0

v1 whole, which is shorter than its diff:
```python
import functools

import jax
import jax.numpy as jnp
from jax import lax
from jax.experimental import pallas as pl
from jax.experimental.pallas import tpu as pltpu
from jax.sharding import PartitionSpec as P

SPAN = 256
HALO = 16
LANES = 128


norm_floor = 0.1


def row_norm(row_block, gain_vector):
    widened = row_block.astype(jnp.float32)
    inverse_rms = lax.rsqrt(jnp.mean(widened * widened, axis=-1, keepdims=True) + norm_floor)
    return widened * inverse_rms * gain_vector


def silu(value):
    return value * (1.0 / (1.0 + jnp.exp(-value)))


def exact_dot(a, b):
    return jnp.dot(a, b, precision=lax.Precision.HIGHEST, preferred_element_type=jnp.float32)


def scan_kernel(
    sizes,
    inner_ref,
    bc_ref,
    dt_ref,
    kernel_x_ref,
    offset_x_ref,
    kernel_bc_ref,
    offset_bc_ref,
    rate_ref,
    skip_ref,
    gain_ref,
    out_ref,
    halo_x,
    halo_bc,
    ext_x,
    ext_bc,
    conv_x,
    conv_bc,
    y_buf,
    cum_buf,
    states,
    carried,
    sum_out,
    sum_in,
    rate_out,
    rate_in,
    carry_out,
    carry_in,
    sq_out,
    sq_in,
    halo_sems,
    sum_send,
    sum_recv,
    rate_send,
    rate_recv,
    carry_send,
    carry_recv,
    sq_send,
    sq_recv,
):
    devices, groups, rows, width, state, taps, head_size = sizes
    blocks = rows // SPAN
    share = state // devices
    total_width = width * groups
    me = lax.axis_index("seq")
    group = lax.axis_index("head")
    seq_peer = [lax.rem(me + o, devices) for o in range(devices)]
    seq_back = [lax.rem(me - o + devices, devices) for o in range(devices)]
    head_peer = [lax.rem(group + o, groups) for o in range(groups)]

    barrier = pltpu.get_barrier_semaphore()
    for o in range(1, devices):
        pl.semaphore_signal(barrier, 1, device_id={"seq": seq_peer[o]})
    for o in range(1, groups):
        pl.semaphore_signal(barrier, 1, device_id={"head": head_peer[o]})
    pl.semaphore_wait(barrier, devices + groups - 2)

    def remote(src, dst, send, recv, axis, peer):
        copy = pltpu.make_async_remote_copy(
            src_ref=src, dst_ref=dst, send_sem=send, recv_sem=recv, device_id={axis: peer}
        )
        return copy

    halo_copies = [
        remote(
            inner_ref.at[pl.ds(rows - HALO, HALO), pl.ds(width, width)],
            halo_x, halo_sems.at[0], halo_sems.at[1], "seq", seq_peer[1],
        ),
        remote(
            bc_ref.at[pl.ds(rows - HALO, HALO), :],
            halo_bc, halo_sems.at[2], halo_sems.at[3], "seq", seq_peer[1],
        ),
    ]
    for copy in halo_copies:
        copy.start()

    def widen(k, carry):
        row = pl.multiple_of(k * 64, 64)
        ext_x[pl.ds(8 + row, 64), :] = inner_ref[pl.ds(row, 64), pl.ds(width, width)].astype(
            jnp.float32
        )
        ext_bc[pl.ds(8 + row, 64), :] = bc_ref[pl.ds(row, 64), :].astype(jnp.float32)
        return carry

    lax.fori_loop(0, rows // 64, widen, 0)
    for copy in halo_copies:
        copy.wait()
    first = me > 0
    ext_x[0:8, :] = jnp.where(first, halo_x[...].astype(jnp.float32)[HALO - 8 :], 0.0)
    ext_bc[0:8, :] = jnp.where(first, halo_bc[...].astype(jnp.float32)[HALO - 8 :], 0.0)

    def convolve(source, weight, bias, target, columns):
        def step(k, carry):
            row = pl.multiple_of(k * 32, 32)
            for lower in range(0, columns, LANES):
                lanes = pl.ds(lower, LANES)
                window = source[pl.ds(row, 40), lanes]
                total = jnp.broadcast_to(bias[0:1, lanes], (32, LANES))
                for tap in range(taps):
                    shift = 8 - taps + 1 + tap
                    total = total + weight[tap : tap + 1, lanes] * window[shift : shift + 32]
                target[pl.ds(row, 32), lanes] = silu(total).astype(jnp.bfloat16)
            return carry

        lax.fori_loop(0, rows // 32, step, 0)

    convolve(ext_bc, kernel_bc_ref, offset_bc_ref, conv_bc, 2 * state)
    convolve(ext_x, kernel_x_ref, offset_x_ref, conv_x, width)

    head_of_lane = lax.broadcasted_iota(jnp.int32, (LANES, width), 1) // head_size
    spread = (head_of_lane == lax.broadcasted_iota(jnp.int32, (LANES, width), 0)).astype(
        jnp.float32
    )
    lower_tri = (
        lax.broadcasted_iota(jnp.int32, (SPAN, SPAN), 0)
        >= lax.broadcasted_iota(jnp.int32, (SPAN, SPAN), 1)
    ).astype(jnp.float32)

    states[0] = jnp.zeros((state, width), jnp.float32)
    prefix = jnp.zeros((1, LANES), jnp.float32)
    prefixes = []
    for block in range(blocks):
        span = pl.ds(block * SPAN, SPAN)
        step_sizes = dt_ref[span, :]
        running = exact_dot(lower_tri, step_sizes * rate_ref[...])
        cum_buf[span, :] = running
        last = running[SPAN - 1 : SPAN, :]
        end_weight = exact_dot(jnp.exp(last - running) * step_sizes, spread)
        scaled = (conv_x[span, :].astype(jnp.float32) * end_weight).astype(jnp.bfloat16)
        new_state = lax.dot_general(
            conv_bc[span, pl.ds(0, state)], scaled, (((0,), (0,)), ((), ())),
            preferred_element_type=jnp.float32,
        )
        decay = exact_dot(jnp.broadcast_to(jnp.exp(last), (8, LANES)), spread)[0:1]
        states[block + 1] = decay * states[block] + new_state
        prefixes.append(prefix)
        prefix = prefix + last

    for j in range(devices):
        sum_out[j] = states[blocks, pl.ds(j * share, share), :].astype(jnp.bfloat16)
    rate_out[...] = jnp.broadcast_to(prefix, (8, LANES))

    row_index = lax.broadcasted_iota(jnp.int32, (LANES, LANES), 0)
    col_index = lax.broadcasted_iota(jnp.int32, (LANES, LANES), 1)
    causal = row_index >= col_index
    lane_index = lax.broadcasted_iota(jnp.int32, (SPAN, LANES), 1)
    pair = LANES // head_size

    def inside(block):
        span = pl.ds(pl.multiple_of(block * SPAN, SPAN), SPAN)
        running = cum_buf[span, :]
        running_t = running.T
        steps_t = dt_ref[span, :].T
        scores = lax.dot_general(
            conv_bc[span, pl.ds(state, state)], conv_bc[span, pl.ds(0, state)],
            (((1,), (1,)), ((), ())), preferred_element_type=jnp.float32,
        )
        half = SPAN // 2
        for strip in range(width // LANES):
            lanes = pl.ds(strip * LANES, LANES)
            value = conv_x[span, lanes]
            upper, bottom, stacked_top, stacked = [], [], [], []
            for member in range(pair):
                head = strip * pair + member
                column = running[:, head : head + 1]
                line = running_t[head : head + 1, :]
                steps = steps_t[head : head + 1, :]

                def weights(r, c):
                    rs, cs = slice(r * half, (r + 1) * half), slice(c * half, (c + 1) * half)
                    gap = column[rs] - line[:, cs]
                    if r == c:
                        gap = jnp.where(causal, gap, -1e30)
                    return (scores[rs, cs] * jnp.exp(gap) * steps[:, cs]).astype(jnp.bfloat16)

                upper.append(weights(0, 0))
                bottom.extend([weights(1, 0), weights(1, 1)])
                own = jnp.where(lane_index // head_size == member, value, jnp.zeros_like(value))
                stacked_top.append(own[:half])
                stacked.append(own)
            top_out = jnp.dot(
                jnp.concatenate(upper, axis=1), jnp.concatenate(stacked_top, axis=0),
                preferred_element_type=jnp.float32,
            )
            bottom_out = jnp.dot(
                jnp.concatenate(bottom, axis=1), jnp.concatenate(stacked, axis=0),
                preferred_element_type=jnp.float32,
            )
            both = jnp.concatenate([top_out, bottom_out], axis=0)
            y_buf[span, lanes] = both + skip_ref[0:1, lanes] * value.astype(jnp.float32)

    sum_copies, rate_copies = [], []
    for o in range(1, devices):
        sum_copies.append(
            remote(
                sum_out.at[seq_peer[o]], sum_in.at[o], sum_send.at[o], sum_recv.at[o],
                "seq", seq_peer[o],
            )
        )
        rate_copies.append(
            remote(
                rate_out, rate_in.at[o], rate_send.at[o], rate_recv.at[o], "seq", seq_peer[o]
            )
        )
    for a, b in zip(sum_copies, rate_copies):
        b.start()
        a.start()

    early = max(blocks - 1, 1)

    def inside_step(block, carry):
        inside(block)
        return carry

    lax.fori_loop(0, early, inside_step, 0)

    for a, b in zip(sum_copies, rate_copies):
        b.wait()
        a.wait()
    sum_in[0] = sum_out[me]
    rate_in[0] = rate_out[...]

    running_state = jnp.zeros((share, width), jnp.float32)
    for i in range(devices):
        slot = lax.rem(me - i + devices, devices)
        carry_out[slot] = running_state.astype(jnp.bfloat16)
        decay = exact_dot(jnp.exp(rate_in[slot]), spread)[0:1]
        running_state = decay * running_state + sum_in[slot].astype(jnp.float32)

    carry_copies = []
    for o in range(1, devices):
        carry_copies.append(
            remote(
                carry_out.at[o], carry_in.at[o], carry_send.at[o], carry_recv.at[o],
                "seq", seq_back[o],
            )
        )
    for copy in carry_copies:
        copy.start()
    lax.fori_loop(early, blocks, inside_step, 0)
    for copy in carry_copies:
        copy.wait()
    carry_in[0] = carry_out[0]
    for j in range(devices):
        slot = lax.rem(j - me + devices, devices)
        carried[pl.ds(j * share, share), :] = carry_in[slot].astype(jnp.float32)

    squares = []
    for block in range(blocks):
        span = pl.ds(block * SPAN, SPAN)
        entry_decay = exact_dot(
            jnp.broadcast_to(jnp.exp(prefixes[block]), (8, LANES)), spread
        )[0:1]
        entering = (states[block] + entry_decay * carried[...]).astype(jnp.bfloat16)
        growth = jnp.exp(cum_buf[span, :])
        partial_sum = jnp.zeros((SPAN, LANES), jnp.float32)
        for strip in range(width // LANES):
            lanes = pl.ds(strip * LANES, LANES)
            column = slice(strip * LANES, (strip + 1) * LANES)
            cross = jnp.dot(
                conv_bc[span, pl.ds(state, state)], entering[:, column],
                preferred_element_type=jnp.float32,
            )
            scale = exact_dot(growth, spread[:, column])
            gated = (y_buf[span, lanes] + scale * cross) * silu(
                inner_ref[span, lanes].astype(jnp.float32)
            )
            y_buf[span, lanes] = gated
            partial_sum = partial_sum + gated * gated
        squares.append(jnp.sum(partial_sum.T, axis=0, keepdims=True))
    own_squares = jnp.concatenate(squares, axis=1)
    sq_out[...] = jnp.broadcast_to(own_squares, (8, rows))
    sq_copies = []
    for o in range(1, groups):
        sq_copies.append(
            remote(sq_out, sq_in.at[o], sq_send.at[o], sq_recv.at[o], "head", head_peer[o])
        )
    for copy in sq_copies:
        copy.start()
    for copy in sq_copies:
        copy.wait()
    total = own_squares
    for o in range(1, groups):
        total = total + sq_in[o, 0:1, :]
    inverse = lax.rsqrt(total / total_width + norm_floor)
    for block in range(blocks):
        part = jnp.broadcast_to(inverse[:, block * SPAN : (block + 1) * SPAN], (LANES, SPAN)).T
        span = pl.ds(block * SPAN, SPAN)
        for strip in range(width // LANES):
            lanes = pl.ds(strip * LANES, LANES)
            out_ref[span, lanes] = (y_buf[span, lanes] * part * gain_ref[0:1, lanes]).astype(
                jnp.bfloat16
            )


def scan_call(inner, bc, step_sizes, kernel_x, offset_x, kernel_bc, offset_bc, rate, skip, gain, head_size):
    devices, groups = lax.axis_size("seq"), lax.axis_size("head")
    rows, width = inner.shape[0], kernel_x.shape[1]
    state, taps = bc.shape[1] // 2, kernel_x.shape[0]
    blocks, share = rows // SPAN, state // devices
    sizes = (devices, groups, rows, width, state, taps, head_size)
    f32, bf16 = jnp.float32, jnp.bfloat16
    sem = pltpu.SemaphoreType.DMA
    return pl.pallas_call(
        functools.partial(scan_kernel, sizes),
        out_shape=jax.ShapeDtypeStruct((rows, width), bf16),
        in_specs=[pl.BlockSpec(memory_space=pltpu.VMEM)] * 10,
        out_specs=pl.BlockSpec(memory_space=pltpu.VMEM),
        scratch_shapes=[
            pltpu.VMEM((HALO, width), bf16),
            pltpu.VMEM((HALO, 2 * state), bf16),
            pltpu.VMEM((rows + 8, width), f32),
            pltpu.VMEM((rows + 8, 2 * state), f32),
            pltpu.VMEM((rows, width), bf16),
            pltpu.VMEM((rows, 2 * state), bf16),
            pltpu.VMEM((rows, width), f32),
            pltpu.VMEM((rows, LANES), f32),
            pltpu.VMEM((blocks + 1, state, width), f32),
            pltpu.VMEM((state, width), f32),
            pltpu.VMEM((devices, share, width), bf16),
            pltpu.VMEM((devices, share, width), bf16),
            pltpu.VMEM((8, LANES), f32),
            pltpu.VMEM((devices, 8, LANES), f32),
            pltpu.VMEM((devices, share, width), bf16),
            pltpu.VMEM((devices, share, width), bf16),
            pltpu.VMEM((8, rows), f32),
            pltpu.VMEM((groups, 8, rows), f32),
            sem((4,)),
            sem((devices,)),
            sem((devices,)),
            sem((devices,)),
            sem((devices,)),
            sem((devices,)),
            sem((devices,)),
            sem((groups,)),
            sem((groups,)),
        ],
        compiler_params=pltpu.CompilerParams(
            collective_id=0, has_side_effects=True, vmem_limit_bytes=60 * 1024 * 1024
        ),
    )(inner, bc, step_sizes, kernel_x, offset_x, kernel_bc, offset_bc, rate, skip, gain)


def on_device(
    tokens,
    pre_gain,
    inner_proj,
    outer_proj,
    kernel_x,
    kernel_bc,
    offset_x,
    offset_bc,
    dt_bias,
    a_log,
    skip_gain,
    norm_gain,
    out_proj,
):
    model_width = inner_proj.shape[0]
    local_width = inner_proj.shape[2]
    head_count = dt_bias.shape[0]
    head_size = local_width // head_count
    state_size = kernel_bc.shape[1] // 2
    joined_proj = inner_proj.reshape(model_width, 2 * local_width)
    normed = row_norm(lax.all_gather(tokens, "head", axis=0, tiled=True), pre_gain).astype(
        jnp.bfloat16
    )
    inner_part = jnp.dot(normed, joined_proj, preferred_element_type=jnp.float32).astype(
        jnp.bfloat16
    )
    outer_part = jnp.dot(normed, outer_proj, preferred_element_type=jnp.float32)
    head_index = lax.axis_index("head")
    dt_raw = lax.dynamic_slice_in_dim(
        outer_part, 2 * state_size + head_index * head_count, head_count, 1
    )
    lane_pad = LANES - head_count
    step_sizes = jnp.pad(jax.nn.softplus(dt_raw + dt_bias), ((0, 0), (0, lane_pad)))
    rate = jnp.pad(-jnp.exp(a_log), (0, lane_pad))[None]
    normed_out = scan_call(
        inner_part,
        outer_part[:, : 2 * state_size].astype(jnp.bfloat16),
        step_sizes,
        kernel_x,
        offset_x[None],
        kernel_bc,
        offset_bc[None],
        rate,
        jnp.repeat(skip_gain, head_size)[None],
        norm_gain[None],
        head_size,
    )
    return lax.psum_scatter(
        jnp.dot(normed_out, out_proj, preferred_element_type=jnp.float32).astype(jnp.bfloat16),
        "head",
        scatter_dimension=0,
        tiled=True,
    )


def solution(mesh):
    return jax.shard_map(
        on_device,
        mesh=mesh,
        in_specs=(
            P(("seq", "head"), None),
            P(),
            P(None, None, "head"),
            P(),
            P(None, "head"),
            P(),
            P("head"),
            P(),
            P("head"),
            P("head"),
            P("head"),
            P("head"),
            P("head", None),
        ),
        out_specs=P(("seq", "head"), None),
        check_vma=False,
    )
```

time: 301 us -> 178 us (0.59)
  waiting for transfers between devices: 132 us -> 62 us
  Pallas kernels: 0 us -> 52.2 us
  local copies, waits for them, and re-layouts: 47.9 us -> 16.9 us
  blocking collectives: 27.6 us -> 0 us
  other arithmetic: 30.4 us -> 3.18 us
  matrix products: 44.2 us -> 29.5 us
  starting transfers between devices: 3.65 us -> 0.04 us
    all_gather x1 -> x0, waiting for transfers between devices: 64.5 us -> none  [entering(): everything = jax.tree.map(lambda part: lax.all_gather(part, axis), array)]
    pallas_call x0 -> x1, Pallas kernels: none -> 52.2 us  [scan_call(): pl.pallas_call(functools.partial(scan_kernel, sizes), out_shape=jax.Shape...]
    reshape x8 -> x0, local copies, waits for them, and re-layouts: 28.5 us -> none  [the longest x2 15.5 us: on_device(): (intra_out + cross_out + skip_gain[:, None] * values_x.astype(jnp.float32...]
    all_gather x1 -> x0, blocking collectives: 21.9 us -> none  [entering(): everything = jax.tree.map(lambda part: lax.all_gather(part, axis), array)]
    dot_general x5 -> x0, matrix products: 16.5 us -> none  [the longest x1 6.64 us: on_device(): jnp.einsum('chts,cshp->cthp', mix_weights, values_x, preferred_element_ty...]
    select_n x8 -> x1, other arithmetic: 9.86 us -> 0.23 us  [on_device(): jax.nn.softplus(dt_raw + dt_bias)]
    convert_element_type x1 -> x0, other arithmetic: 7.02 us -> none  [on_device(): conv_out = jax.nn.silu(summed).astype(jnp.bfloat16)]
    psum x1 -> x0, blocking collectives: 5.67 us -> none  [on_device(): squares = lax.psum(jnp.sum(gated * gated, axis=1), 'head')]
  transfers between devices with their start and end apart: 4 -> 2, of which waited for: 4 -> 2; matrix products, arithmetic and copies ran while one was open for 4% -> 8% of each run, Pallas kernels for 0% -> 0%
where the time goes in v1:
time: 178 us; the launch traced here: 177 us
  waiting for transfers between devices  62 us (35%)
  Pallas kernels  52.2 us (29%)
  matrix products  29.5 us (17%)
  local copies, waits for them, and re-layouts  16.9 us (9%)
  between operations  13.5 us (8%)
  other arithmetic  3.18 us (2%)
    pallas_call x1, Pallas kernels, scan_call(): pl.pallas_call(functools.partial(scan_kernel, sizes), out_shape=jax.Shape...  52.2 us
    reduce_scatter x1, waiting for transfers between devices, on_device(): lax.psum_scatter(jnp.dot(normed_out, out_proj, preferred_element_type=jnp...  39 us
    all_gather x1, waiting for transfers between devices, on_device(): lax.all_gather(tokens, 'head', axis=0, tiled=True)  22.3 us
    dot_general x1, matrix products, on_device(): jnp.dot(normed, joined_proj, preferred_element_type=jnp.float32)  15.9 us
    unnamed x17, local copies, waits for them, and re-layouts  13.6 us
    dot_general x1, matrix products, on_device(): jnp.dot(normed_out, out_proj, preferred_element_type=jnp.float32)  9.86 us
    dot_general x1, matrix products, on_device(): outer_part = jnp.dot(normed, outer_proj, preferred_element_type=jnp.float32)  3.72 us
  transfers between devices with their start and end apart: 2, of which 2 were waited for; matrix products, arithmetic and copies ran while one was open for 8% of the time, Pallas kernels for 0%

profile of v1, /device:TPU:0, one launch (start us, length us, event | category | flops | bytes accessed | tf_op | source)
XLA Modules:
  0.0 177.4 jit_solution(4376624075152696982)
XLA Ops:
  6.5 0.0 copy-start
  6.5 0.0 all-gather.2.cloned.1.call-start
  6.5 0.7 all-gather.2.cloned.1.call-update
  7.3 0.0 reduce-scatter.2.cloned.1.call-start
  7.3 0.0 copy-start.1
  7.3 0.0 copy-start.3
  7.3 0.0 copy-start.2
  7.3 0.0 copy-start.6
  7.3 0.0 copy-start.5
  7.4 12.4 %copy.20 = bf16[320,8,2,1280]{3,1,2,0:T(8,128)(2,1)} copy(bf16[320,8,2,1280]{3,2,1,0:T(2,128)(2,1)} %bitcast.9) | data formatting | bytes 26214400
  19.8 0.0 copy-done.1
  19.8 0.6 broadcast_in_dim.18.offset_x_ref
  20.4 0.0 copy-done.3
  20.4 0.1 broadcast_in_dim.21
  20.5 0.7 broadcast_in_dim_reshape.3.skip_ref
  21.2 0.0 copy-done.2
  21.2 0.6 broadcast_in_dim.22.gain_ref
  21.8 0.0 copy-done.6
  21.8 0.6 pad_bitcast_fusion.rate_ref
  22.3 22.3 %all-gather.2.cloned.1.call-done = bf16[768,2560]{1,0:T(8,128)(2,1)} async-done(((bf16[192,2560]{1,0:T(8,128)(2,1)}), bf16[768,2560]{1,0:T(8,128)(2,1)}) %all-gather.2.cloned.1.call-update) | async-done | bytes 3932176 | tf_op jit(solution)/shard_map/all_gather | solution.py:397
  44.6 2.9 %fusion = f32[768]{0:T(1024)S(1)} fusion(bf16[768,2560]{1,0:T(8,128)(2,1)} %all-gather.2.cloned.1.call-done), kind=kLoop, calls=%fused_computation.2 | loop fusion | flops 5897472 | bytes 3935232 | tf_op jit(solution)/shard_map/reduce_sum | solution.py:20
  47.6 0.0 copy-start.4
  47.6 3.7 %fusion.3 = f32[768,336]{0,1:T(8,128)S(1)} fusion(bf16[2560,336]{0,1:T(8,128)(2,1)S(1)} %copy-done, bf16[768,2560]{1,0:T(8,128)(2,1)} %all-gather.2.cloned.1.call-done, f32[2560]{0:T(1024)S(1)} %copy-done.5, f32[768]{0:T(1024)S(1)} %add_rsqrt_fusion), kind=kOutput, calls=%fused_computation.8 | convolution fusion | flops 1329070080 | bytes 6697984 | tf_op jit(solution)/shard_map/dot_general | solution.py:403
  51.4 0.9 copy.18.bc_ref
  52.3 0.2 copy.19
  52.5 0.2 compare_select_fusion
  52.7 0.8 pad.8.dt_ref
  53.5 15.9 %convolution_convert_fusion.1.inner_ref = bf16[768,2560]{1,0:T(8,128)(2,1)} fusion(bf16[2560,2560]{1,0:T(8,128)(2,1)} %bitcast.10, bf16[768,2560]{1,0:T(8,128)(2,1)} %all-gather.2.cloned.1.call-done, f32[2560]{0:T(1024)S(1)} %copy-done.5, f32[768]{0:T(1024)S(1)} %add_rsqrt_fusion), kind=kOutput, calls=%fused_computation.6 | convolution fusion | flops 10076160000 | bytes 20984832 | tf_op jit(solution)/shard_map/dot_general | solution.py:400
  69.4 52.2 %shard_map.127 = bf16[768,1280]{1,0:T(8,128)(2,1)} custom-call(bf16[768,2560]{1,0:T(8,128)(2,1)} %convolution_convert_fusion.1.inner_ref, bf16[768,256]{1,0:T(8,128)(2,1)} %copy.18.bc_ref, f32[768,128]{1,0:T(8,128)} %pad.8.dt_ref, f32[4,1280]{1,0:T(4,128)} %kernel_x_ref.1, f32[1,1280]{1,0:T(1,128)} %broadcast_in_dim.18.offset_x_ref, f32[4,256]{1,0:T(4,128)} %kernel_bc_ref.1, ...), custom_call_target="tpu_custom_call" | custom-call | tf_op jit(solution)/shard_map/pallas_call | solution.py:336
  121.7 9.9 %convolution_convert_fusion = bf16[768,2560]{1,0:T(8,128)(2,1)} fusion(bf16[768,1280]{1,0:T(8,128)(2,1)} %shard_map.127, bf16[1280,2560]{1,0:T(8,128)(2,1)} %param.25), kind=kOutput, calls=%fused_computation.5 | convolution fusion | flops 5035130880 | bytes 12451840 | tf_op jit(solution)/shard_map/dot_general | solution.py:425
  131.5 0.0 reduce-scatter.2.cloned.1.call-update
  131.5 39.0 %reduce-scatter.2.cloned.1.call-done = bf16[192,2560]{1,0:T(8,128)(2,1)} async-done(((bf16[768,2560]{1,0:T(8,128)(2,1)}), bf16[192,2560]{1,0:T(8,128)(2,1)}) %reduce-scatter.2.cloned.1.call-update) | async-done | bytes 983056 | tf_op jit(solution)/shard_map/reduce_scatter | solution.py:424
  (7 shorter events, 0.1 us)
Async XLA Ops:
  6.5 41.0 %copy-start = (bf16[2560,336]{0,1:T(8,128)(2,1)S(1)}, bf16[2560,336]{0,1:T(8,128)(2,1)}, u32[]{:S(2)}) copy-start(bf16[2560,336]{0,1:T(8,128)(2,1)} %param.16) | copy-start | bytes 5160964
  6.5 38.1 %all-gather.2.cloned.1.call-start = ((), (), s32[]{:S(2)}) async-start(), calls=%async_computation.1 | async-start | bytes 4915200 | tf_op jit(solution)/shard_map/all_gather | solution.py:397
  7.3 163.3 %reduce-scatter.2.cloned.1.call-start = ((), (), s32[]{:S(2)}) async-start(), calls=%async_computation.2 | async-start | bytes 4915200 | tf_op jit(solution)/shard_map/reduce_scatter | solution.py:424
  7.3 12.5 %copy-start.1 = (f32[1280]{0:T(1024)S(1)}, f32[1280]{0:T(1024)}, u32[]{:S(2)}) copy-start(f32[1280]{0:T(1024)} %param.19) | copy-start | bytes 15364
  7.3 13.1 %copy-start.3 = (f32[20]{0:T(128)S(1)}, f32[20]{0:T(128)}, u32[]{:S(2)}) copy-start(f32[20]{0:T(128)} %param.23) | copy-start | bytes 244
  7.3 13.8 %copy-start.2 = (f32[1280]{0:T(1024)S(1)}, f32[1280]{0:T(1024)}, u32[]{:S(2)}) copy-start(f32[1280]{0:T(1024)} %param.24) | copy-start | bytes 15364
  7.3 14.4 %copy-start.6 = (f32[20]{0:T(128)S(1)}, f32[20]{0:T(128)}, u32[]{:S(2)}) copy-start(f32[20]{0:T(128)} %param.22) | copy-start | bytes 244
  7.3 40.2 %copy-start.5 = (f32[2560]{0:T(1024)S(1)}, f32[2560]{0:T(1024)}, u32[]{:S(2)}) copy-start(f32[2560]{0:T(1024)} %param.14) | copy-start | bytes 30724
  47.6 4.9 %copy-start.4 = (f32[20]{0:T(128)S(1)}, f32[20]{0:T(128)}, u32[]{:S(2)}) copy-start(f32[20]{0:T(128)} %param.21) | copy-start | bytes 244
Sparse Core Ops, SparseCore 0:
  8.9 35.6 all-gather.1
  131.7 38.8 reduce-scatter.1
